TPU v7x, 256 devices: a whole 4x4x8 slice. The times are simulated.
256 devices in a mesh: ens: 2 (over y_hi), time: 32 (over z, x), chan: 4 (over y_lo, core).
Axes of the slice: x: 4, y: 4 (y_hi: 2, y_lo: 2; y = y_hi * 2 + y_lo), z: 8, core: 2. Of those that a mesh axis runs over, the one named last changes fastest.
Arguments:
- decay_rate: float32 [4, 32768, 1024], P('ens', 'time', 'chan'), parts along dimension 0, may hold values from 0.2 to 2
- drive_in: bfloat16 [4, 32768, 1024], P('ens', 'time', 'chan'), parts along dimension 0, may hold values from -6 to 6
- gate_in: bfloat16 [4, 32768, 1024], P('ens', 'time', 'chan'), parts along dimension 0, may hold values from -6 to 6
- norm_gain: float32 [2048], P(('ens', 'chan')), parts along dimension 0, may hold values from 0.25 to 1.75
Outputs:
- mixed_out: bfloat16 [4, 32768, 1024], P('ens', 'time', 'chan'), parts along dimension 0
There are 2 independent parts, one for each index of `ens`. A program takes and returns all parts, laid end to end along the dimension named above; each array names one. Nothing has to cross between parts.
All inputs are finite; a program needn't handle non-finite values.
Results may differ from a plain program's by a relative error of at most 0.001.
Values sent between devices are 32-bit elements.
A program may use at most 64 MiB of HBM per device.

v0:
```python
import jax
import jax.numpy as jnp
from jax import lax
from jax.sharding import Mesh
from jax.sharding import PartitionSpec as P

TIME = ("time_0", "time_1")


def neutral_like(value, identity):
    return jax.tree.map(
        lambda a, e: jnp.broadcast_to(jnp.asarray(e, a.dtype), a.shape), value, identity
    )


def carried_in(value, axes, combine, identity, reverse):
    before = start = neutral_like(value, identity)
    running = value
    for axis in reversed(axes):
        devices, position = lax.axis_size(axis), lax.axis_index(axis)
        pieces = jax.tree.map(lambda part: lax.all_gather(part, axis), running)
        inside, running = start, start
        for k in reversed(range(devices)) if reverse else range(devices):
            passed = k > position if reverse else k < position
            running = combine(running, jax.tree.map(lambda part: part[k], pieces))
            inside = jax.tree.map(lambda new, old: jnp.where(passed, new, old), running, inside)
        before = combine(inside, before)
    return before


def over_pieces(value, axis):
    parts = lax.all_gather(value, axis)
    return parts.sum(axis=0)


def join_pair(earlier, later):
    return (earlier[0] * later[0], later[0] * earlier[1] + later[1])


def on_device(decay_rate, drive_in, gate_in, norm_gain):
    total_length = decay_rate.shape[1] * lax.axis_size(TIME)
    keep = jnp.exp(-decay_rate / total_length)
    push = drive_in.astype(jnp.float32) * total_length ** (-0.5)
    steps = -decay_rate / total_length
    logs = jnp.sum(steps, axis=1, keepdims=True) - jnp.cumsum(steps, axis=1)
    later_logs = logs
    summary = (jnp.exp(jnp.sum(steps, axis=1)), jnp.sum(jnp.exp(later_logs) * push, axis=1))
    entering_forward = carried_in(
        summary, TIME, join_pair, (jnp.ones_like(keep[:, 0]), jnp.zeros_like(push[:, 0])), False
    )
    started = push.at[:, 0].add(keep[:, 0] * entering_forward[1])
    forward = lax.associative_scan(join_pair, (keep, started), axis=1)[1]
    steps = -decay_rate / total_length
    logs = jnp.cumsum(steps, axis=1)
    before_logs = logs - steps
    summary = (jnp.exp(logs[:, -1]), jnp.sum(jnp.exp(before_logs) * push, axis=1))
    entering_backward = carried_in(
        summary, TIME, join_pair, (jnp.ones_like(keep[:, 0]), jnp.zeros_like(push[:, 0])), True
    )
    started = push.at[:, -1].add(keep[:, -1] * entering_backward[1])
    backward = lax.associative_scan(join_pair, (keep, started), axis=1, reverse=True)[1]
    states = forward + backward
    gated = states * jax.nn.silu(gate_in.astype(jnp.float32))
    power = over_pieces(jnp.sum(gated * gated, axis=-1, keepdims=True), "chan") / (
        gated.shape[-1] * lax.axis_size("chan")
    )
    mixed_out = (gated * lax.rsqrt(power + 1e-06) * norm_gain).astype(jnp.bfloat16)
    return mixed_out


def solution(mesh):
    finer = Mesh(
        mesh.devices.reshape(mesh.shape["ens"], 8, 4, mesh.shape["chan"]),
        ("ens", "time_0", "time_1", "chan"),
    )
    in_specs = (
        P("ens", TIME, "chan"),
        P("ens", TIME, "chan"),
        P("ens", TIME, "chan"),
        P(("ens", "chan")),
    )
    out_specs = P("ens", TIME, "chan")
    return jax.shard_map(
        on_device, mesh=finer, in_specs=in_specs, out_specs=out_specs, check_vma=False
    )
```

profile of v0, /device:TPU:1, one launch (start us, length us, event | category | flops | bytes accessed | tf_op | source)
XLA Modules:
  0.0 363.0 jit_solution(3151391685839674871)
XLA Ops:
  3.2 10.1 %all-gather.5 = f32[4,2,256]{2,1,0:T(2,128)S(1)} all-gather(f32[1,2,256]{2,1,0:T(2,128)S(1)} %exponential_bitcast_fusion), channel_id=2, replica_groups=mesh['ens'=2,'time_0'=8,'time_1'=4,'chan'=4] {'time_1'}, dimensions={0}, use_global_device_ids=true | all-gather | bytes 10240 | tf_op jit(solution)/shard_map/all_gather | solution.py:21
  17.1 8.9 %all-gather.2 = f32[8,1,256]{2,1,0:T(1,128)S(1)} all-gather(f32[2,1,256]{2,1,0:T(1,128)S(1)} %slice_exponential_fusion), channel_id=4, replica_groups=mesh['ens'=2,'time_0'=8,'time_1'=4,'chan'=4] {'time_1'}, dimensions={0}, use_global_device_ids=true | all-gather | bytes 10240 | tf_op jit(solution)/shard_map/all_gather | solution.py:21
  30.8 8.9 %slice.813 = f32[2,512,256]{2,1,0:T(8,128)} reverse(f32[2,512,256]{2,1,0:T(8,128)} %slice.705), dimensions={1} | reverse | bytes 2097152 | tf_op jit(solution)/shard_map/slice | solution.py:61
  39.7 5.2 %slice.807 = f32[2,512,256]{2,1,0:T(8,128)} reverse(f32[2,512,256]{2,1,0:T(8,128)S(1)} %slice.709), dimensions={1} | reverse | bytes 2097152 | tf_op jit(solution)/shard_map/slice | solution.py:61
  48.4 9.1 %slice.806 = f32[2,511,256]{2,1,0:T(8,128)} reverse(f32[2,511,256]{2,1,0:T(8,128)} %slice.805), dimensions={1} | reverse | bytes 2093056 | tf_op jit(solution)/shard_map/slice | solution.py:61
  64.6 8.9 %all-gather.7 = f32[4,2,256]{2,1,0:T(2,128)S(1)} all-gather(f32[1,2,256]{2,1,0:T(2,128)S(1)} %bitcast.179), channel_id=5, replica_groups=mesh['ens'=2,'time_0'=8,'time_1'=4,'chan'=4] {'time_1'}, dimensions={0}, use_global_device_ids=true | all-gather | bytes 10240 | tf_op jit(solution)/shard_map/all_gather | solution.py:21
  73.6 8.9 %all-gather.6 = f32[4,2,256]{2,1,0:T(2,128)S(1)} all-gather(f32[1,2,256]{2,1,0:T(2,128)S(1)} %bitcast.178), channel_id=3, replica_groups=mesh['ens'=2,'time_0'=8,'time_1'=4,'chan'=4] {'time_1'}, dimensions={0}, use_global_device_ids=true | all-gather | bytes 10240 | tf_op jit(solution)/shard_map/all_gather | solution.py:21
  82.6 21.8 %all_gather.43 = f32[8,2,256]{2,1,0:T(2,128)S(1)} all-gather(f32[1,2,256]{2,1,0:T(2,128)S(1)} %copy.27), channel_id=1, replica_groups=mesh['ens'=2,'time_0'=8,'time_1'=4,'chan'=4] {'time_0'}, dimensions={0}, use_global_device_ids=true | all-gather | bytes 18432 | tf_op jit(solution)/shard_map/all_gather | solution.py:21
  104.3 18.1 %all_gather.40 = f32[8,2,256]{2,1,0:T(2,128)S(1)} all-gather(f32[1,2,256]{2,1,0:T(2,128)S(1)} %copy.12), channel_id=1, replica_groups=mesh['ens'=2,'time_0'=8,'time_1'=4,'chan'=4] {'time_0'}, dimensions={0}, use_global_device_ids=true | all-gather | bytes 18432 | tf_op jit(solution)/shard_map/all_gather | solution.py:21
  123.2 18.1 %all_gather.48 = f32[8,2,256]{2,1,0:T(2,128)S(1)} all-gather(f32[1,2,256]{2,1,0:T(2,128)S(1)} %copy.49), channel_id=1, replica_groups=mesh['ens'=2,'time_0'=8,'time_1'=4,'chan'=4] {'time_0'}, dimensions={0}, use_global_device_ids=true | all-gather | bytes 18432 | tf_op jit(solution)/shard_map/all_gather | solution.py:21
  141.4 18.1 %all_gather.45 = f32[8,2,256]{2,1,0:T(2,128)S(1)} all-gather(f32[1,2,256]{2,1,0:T(2,128)S(1)} %copy.36), channel_id=1, replica_groups=mesh['ens'=2,'time_0'=8,'time_1'=4,'chan'=4] {'time_0'}, dimensions={0}, use_global_device_ids=true | all-gather | bytes 18432 | tf_op jit(solution)/shard_map/all_gather | solution.py:21
  163.2 6.5 %slice.777 = f32[2,511,256]{2,1,0:T(8,128)} slice(f32[2,1024,256]{2,1,0:T(8,128)} %scatter-add.6), slice={[0:2:1], [2:1024:2], [0:256:1]} | slice | bytes 2093056 | tf_op jit(solution)/shard_map/slice | solution.py:52
  169.7 6.4 %slice.707 = f32[2,512,256]{2,1,0:T(8,128)} slice(f32[2,1024,256]{2,1,0:T(8,128)} %scatter-add.6), slice={[0:2:1], [1:1024:2], [0:256:1]} | slice | bytes 2097152 | tf_op jit(solution)/shard_map/slice | solution.py:52
  176.1 6.4 %slice.706 = f32[2,512,256]{2,1,0:T(8,128)} slice(f32[2,1024,256]{2,1,0:T(8,128)} %scatter-add.6), slice={[0:2:1], [0:1023:2], [0:256:1]} | slice | bytes 2097152 | tf_op jit(solution)/shard_map/slice | solution.py:52
  186.7 4.2 %slice.715 = f32[2,256,256]{2,1,0:T(8,128)} slice(f32[2,512,256]{2,1,0:T(8,128)} %get-tuple-element.36), slice={[0:2:1], [0:511:2], [0:256:1]} | slice | bytes 1048576 | tf_op jit(solution)/shard_map/slice | solution.py:52
  190.9 4.1 %slice.711 = f32[2,256,256]{2,1,0:T(8,128)} slice(f32[2,512,256]{2,1,0:T(8,128)} %get-tuple-element.36), slice={[0:2:1], [1:512:2], [0:256:1]} | slice | bytes 1048576 | tf_op jit(solution)/shard_map/slice | solution.py:52
  195.0 4.2 %slice.710 = f32[2,255,256]{2,1,0:T(8,128)} slice(f32[2,512,256]{2,1,0:T(8,128)} %get-tuple-element.36), slice={[0:2:1], [2:512:2], [0:256:1]} | slice | bytes 1044480 | tf_op jit(solution)/shard_map/slice | solution.py:52
  230.3 5.3 %pad.144 = f32[2,1024,256]{2,1,0:T(8,128)} pad(f32[2,512,256]{2,1,0:T(8,128)} %pad_maximum_fusion, f32[]{:T(128)} %constant.88.clone.1), padding=0_0_0x0_1_1x0_0_0 | pad | bytes 3145732 | tf_op jit(solution)/shard_map/pad | solution.py:52
  240.2 5.4 %slice.882 = f32[2,511,256]{2,1,0:T(8,128)} reverse(f32[2,511,256]{2,1,0:T(8,128)S(1)} %slice.881), dimensions={1} | reverse | bytes 2093056 | tf_op jit(solution)/shard_map/slice | solution.py:61
  250.4 8.9 %slice.809 = f32[2,512,256]{2,1,0:T(8,128)} reverse(f32[2,512,256]{2,1,0:T(8,128)} %slice.808), dimensions={1} | reverse | bytes 2097152 | tf_op jit(solution)/shard_map/slice | solution.py:61
  259.3 5.2 %slice.811 = f32[2,512,256]{2,1,0:T(8,128)} reverse(f32[2,512,256]{2,1,0:T(8,128)S(1)} %slice.810), dimensions={1} | reverse | bytes 2097152 | tf_op jit(solution)/shard_map/slice | solution.py:61
  296.2 16.8 %rev.2 = f32[2,1024,256]{2,1,0:T(8,128)} reverse(f32[2,1024,256]{2,1,0:T(8,128)} %add.621), dimensions={1} | reverse | bytes 4194304 | tf_op jit(solution)/shard_map/rev | solution.py:61
  313.0 4.3 %multiply_reduce_fusion = (f32[2,1024]{1,0:T(2,128)S(1)}, f32[2,1024,256]{2,1,0:T(8,128)}) fusion(bf16[2,1024,256]{2,1,0:T(8,128)(2,1)S(1)} %copy-done.10, f32[2,1024,256]{2,1,0:T(8,128)} %rev.2, f32[2,1024,256]{2,1,0:T(8,128)S(1)} %copy-done.4, f32[2,1024,256]{2,1,0:T(8,128)} %pad.145), kind=kLoop, calls=%fused_computation.9 | loop fusion | flops 5240832 | bytes 9445376 | tf_op jit(solution)/shard_map/reduce_sum | solution.py:64
  317.3 42.7 %all-gather.8 = f32[4,2,1024]{2,1,0:T(2,128)S(1)} all-gather(f32[1,2,1024]{2,1,0:T(2,128)S(1)} %bitcast.177), channel_id=6, replica_groups=mesh['ens'=2,'time_0'=8,'time_1'=4,'chan'=4] {'chan'}, dimensions={0}, use_global_device_ids=true | all-gather | bytes 40960 | tf_op jit(solution)/shard_map/all_gather | solution.py:32
  (277 shorter events, 105.3 us)
Async XLA Ops:
  1.9 55.7 %copy-start = (f32[2,1024,256]{2,1,0:T(8,128)}, f32[2,1024,256]{2,1,0:T(8,128)S(1)}, u32[]{:S(2)}) copy-start(f32[2,1024,256]{2,1,0:T(8,128)S(1)} %get-tuple-element.33) | copy-start | bytes 6291460
  3.2 10.1 %copy-start.2 = (f32[2,256,8,128]{1,2,3,0:T(8,128)}, f32[2,256,8,128]{1,2,3,0:T(8,128)S(1)}, u32[]{:S(2)}) copy-start(f32[2,256,8,128]{1,2,3,0:T(8,128)S(1)} %fusion.4) | copy-start | bytes 6291460
  15.8 1.3 copy-start.3
  185.7 1.0 copy-start.5
  186.7 12.5 %copy-start.6 = (f32[2,512,256]{2,1,0:T(8,128)S(1)}, f32[2,512,256]{2,1,0:T(8,128)}, u32[]{:S(2)}) copy-start(f32[2,512,256]{2,1,0:T(8,128)} %copy-done.5) | copy-start | bytes 3145732
  216.1 1.1 copy-start.11
  225.8 2.2 copy-start.1
  230.3 5.3 %copy-start.8 = (f32[2,512,256]{2,1,0:T(8,128)S(1)}, f32[2,512,256]{2,1,0:T(8,128)}, u32[]{:S(2)}) copy-start(f32[2,512,256]{2,1,0:T(8,128)} %add.571) | copy-start | bytes 3145732
  270.5 5.0 %copy-start.9 = (f32[2,256,256]{2,1,0:T(8,128)S(1)}, f32[2,256,256]{2,1,0:T(8,128)}, u32[]{:S(2)}) copy-start(f32[2,256,256]{2,1,0:T(8,128)} %slice.815) | copy-start | bytes 1572868
  283.0 1.5 copy-start.7
  296.2 16.8 %copy-start.4 = (f32[2,1024,256]{2,1,0:T(8,128)S(1)}, f32[2,1024,256]{2,1,0:T(8,128)}, u32[]{:S(2)}) copy-start(f32[2,1024,256]{2,1,0:T(8,128)} %pad.144) | copy-start | bytes 6291460
  296.2 16.8 %copy-start.10 = (bf16[2,1024,256]{2,1,0:T(8,128)(2,1)S(1)}, bf16[2,1024,256]{2,1,0:T(8,128)(2,1)}, u32[]{:S(2)}) copy-start(bf16[2,1024,256]{2,1,0:T(8,128)(2,1)} %param.10) | copy-start | bytes 3145732
  313.0 47.1 %copy-start.12 = (f32[256]{0:T(256)S(1)}, f32[256]{0:T(256)}, u32[]{:S(2)}) copy-start(f32[256]{0:T(256)} %param.11) | copy-start | bytes 3076
where the time goes:
time: 367 us; the launch traced here: 363 us
  local copies, waits for them, and re-layouts  161 us (44%)
  blocking collectives  156 us (43%)
  other arithmetic  45.1 us (12%)
    all_gather x8, blocking collectives, carried_in(): pieces = jax.tree.map(lambda part: lax.all_gather(part, axis), running)  113 us
    slice x63, local copies, waits for them, and re-layouts, on_device(): lax.associative_scan(join_pair, (keep, started), axis=1, reverse=True)[1]  63.3 us
    slice x59, local copies, waits for them, and re-layouts, on_device(): forward = lax.associative_scan(join_pair, (keep, started), axis=1)[1]  53.6 us
    all_gather x1, blocking collectives, over_pieces(): parts = lax.all_gather(value, axis)  42.7 us
    rev x1, local copies, waits for them, and re-layouts, on_device(): lax.associative_scan(join_pair, (keep, started), axis=1, reverse=True)[1]  16.8 us
    pad x18, local copies, waits for them, and re-layouts, on_device(): forward = lax.associative_scan(join_pair, (keep, started), axis=1)[1]  13.5 us
    mul x18, other arithmetic, join_pair(): return (earlier[0] * later[0], later[0] * earlier[1] + later[1])  12 us
    pad x18, local copies, waits for them, and re-layouts, on_device(): lax.associative_scan(join_pair, (keep, started), axis=1, reverse=True)[1]  7.84 us

commit v1 on v0

v1 whole, which is shorter than its diff:
```python
import functools

import jax
import jax.numpy as jnp
from jax import lax
from jax.experimental import pallas as pl
from jax.experimental.pallas import tpu as pltpu
from jax.sharding import PartitionSpec as P

F32, BF16 = jnp.float32, jnp.bfloat16
BLOCK = 256
CHUNK = 32
LANES = 128


def dot(a, b):
    return lax.dot_general(a, b, (((1,), (0,)), ((), ())), preferred_element_type=F32)


def peers_by_distance(count, width):
    rows = count // width
    away = lambda s, n: min(s, n - s)
    shifts = [(r, c) for r in range(rows) for c in range(width) if r or c]
    return sorted(shifts, key=lambda s: -(away(s[0], rows) + away(s[1], width)))


def kernel(
    times, chans, width,
    decay_hbm, drive_hbm, gate_hbm, gain_ref, out_hbm,
    decay, drive, gate, cum, up, down, base, into, back, result,
    note, notes, entry, power, powers,
    in_sem, out_sem, time_send, time_recv, chan_send, chan_recv,
):
    batch, length, channels = decay.shape
    blocks = length // BLOCK
    each = [(b, k) for b in range(batch) for k in range(blocks)]
    rows_of = lambda k: pl.ds(k * BLOCK, BLOCK)
    per_length = 1.0 / (length * times)
    t_me, c_me = lax.axis_index("time"), lax.axis_index("chan")
    row, column = t_me // width, t_me % width
    tall = times // width
    t_peers = [
        ((row + r) % tall) * width + (column + c) % width
        for r, c in peers_by_distance(times, width)
    ]
    c_peers = [(c_me + s) % chans for s in range(1, chans)]

    barrier = pltpu.get_barrier_semaphore()
    for peer in t_peers:
        pl.semaphore_signal(barrier, 1, device_id={"time": peer})
    for peer in c_peers:
        pl.semaphore_signal(barrier, 1, device_id={"chan": peer})

    def fetch(which, b, k):
        source, target = ((decay_hbm, decay), (drive_hbm, drive), (gate_hbm, gate))[which]
        return pltpu.make_async_copy(
            source.at[b, rows_of(k), :], target.at[b, rows_of(k), :], in_sem.at[which, b * blocks + k]
        )

    for b, k in each:
        fetch(0, b, k).start()
        fetch(1, b, k).start()
    for b, k in each:
        fetch(2, b, k).start()

    iota = lambda d: lax.broadcasted_iota(jnp.int32, (BLOCK, BLOCK), d)
    lower = jnp.where(iota(0) >= iota(1), 1.0, 0.0).astype(BF16)
    upper = jnp.where(iota(0) <= iota(1), 1.0, 0.0).astype(BF16)

    shrink, gain_up, gain_down = {}, {}, {}
    for b, k in each:
        fetch(0, b, k).wait()
        whole = decay[b, rows_of(k), :]
        high = whole.astype(BF16)
        low = (whole - high.astype(F32)).astype(BF16)
        cum[b, rows_of(k), :] = dot(lower, high) + dot(lower, low)
        fetch(1, b, k).wait()
        plain = rising = falling = jnp.zeros((8, channels), F32)
        for r in range(0, BLOCK, CHUNK):
            at = pl.ds(k * BLOCK + r, CHUNK)
            logs = cum[b, at, :] * per_length
            step = decay[b, at, :] * per_length
            push = drive[b, at, :].astype(F32)
            u = push * (jnp.exp(logs) - 1.0)
            v = push * (jnp.exp(step - logs) - 1.0)
            up[b, at, :] = u.astype(BF16)
            down[b, at, :] = v.astype(BF16)
            fold = lambda a: jnp.sum(a.reshape(CHUNK // 8, 8, channels), axis=0)
            plain, rising, falling = plain + fold(push), rising + fold(u), falling + fold(v)
        total = lambda a: jnp.sum(a, axis=0, keepdims=True)
        shrink[b, k] = jnp.exp(cum[b, pl.ds((k + 1) * BLOCK - 1, 1), :] * -per_length)
        gain_up[b, k] = total(plain + rising)
        gain_down[b, k] = total(plain + falling)

    for b in range(batch):
        kept = shrink[b, 0]
        ahead = shrink[b, 0] * gain_up[b, 0]
        for k in range(1, blocks):
            kept = kept * shrink[b, k]
            ahead = shrink[b, k] * (ahead + gain_up[b, k])
        behind = gain_down[b, blocks - 1]
        for k in reversed(range(blocks - 1)):
            behind = shrink[b, k] * behind + gain_down[b, k]
        for h in range(channels // LANES):
            lanes = slice(h * LANES, (h + 1) * LANES)
            r = b * (channels // LANES) + h
            for way, state in ((0, ahead), (1, behind)):
                note[way, r : r + 1, :] = kept[:, lanes]
                note[way, 4 + r : 5 + r, :] = state[:, lanes]

    pl.semaphore_wait(barrier, len(t_peers) + len(c_peers))

    def tell(peer):
        return pltpu.make_async_remote_copy(
            src_ref=note.at[jnp.where(peer > t_me, 0, 1)],
            dst_ref=notes.at[t_me],
            send_sem=time_send.at[peer],
            recv_sem=time_recv.at[t_me],
            device_id={"time": peer},
        )

    def told(peer):
        return pltpu.make_async_remote_copy(
            src_ref=note.at[0],
            dst_ref=notes.at[peer],
            send_sem=time_send.at[peer],
            recv_sem=time_recv.at[peer],
            device_id={"time": peer},
        )

    for peer in t_peers:
        tell(peer).start()
    notes[t_me] = note[0]

    for b, k in each:
        push = drive[b, rows_of(k), :]
        base[b, rows_of(k), :] = dot(lower, push) + dot(lower, up[b, rows_of(k), :])
        into[b, rows_of(k), :] = dot(upper, push) + dot(upper, down[b, rows_of(k), :])
        fetch(2, b, k).wait()
        for r in range(0, BLOCK, CHUNK):
            at = pl.ds(k * BLOCK + r, CHUNK)
            logs = cum[b, at, :] * per_length
            step = decay[b, at, :] * per_length
            g = gate[b, at, :].astype(F32)
            g = g * ((length * times) ** -0.5) / (1.0 + jnp.exp(-g))
            p, q = g * jnp.exp(-logs), g * jnp.exp(logs - step)
            base[b, at, :] = p * base[b, at, :] + q * into[b, at, :]
            into[b, at, :] = p
            back[b, at, :] = q

    for peer in t_peers:
        told(peer).wait_recv()
    ahead = behind = jnp.zeros((8, LANES), F32)
    for t in range(times):
        one = notes[t]
        ahead = jnp.where(t < t_me, ahead * pltpu.roll(one, 4, 0) + one, ahead)
        one = notes[times - 1 - t]
        behind = jnp.where(times - 1 - t > t_me, behind * pltpu.roll(one, 4, 0) + one, behind)
    entry[0] = ahead
    entry[1] = behind

    lane = lax.broadcasted_iota(jnp.int32, (CHUNK, LANES), 1)
    group = lax.broadcasted_iota(jnp.int32, (CHUNK, LANES), 0) // 8

    def share(b, peer):
        return pltpu.make_async_remote_copy(
            src_ref=power.at[b],
            dst_ref=powers.at[c_me, b],
            send_sem=chan_send.at[peer, b],
            recv_sem=chan_recv.at[c_me, b],
            device_id={"chan": peer},
        )

    def shared(b, peer):
        return pltpu.make_async_remote_copy(
            src_ref=power.at[b],
            dst_ref=powers.at[peer, b],
            send_sem=chan_send.at[peer, b],
            recv_sem=chan_recv.at[peer, b],
            device_id={"chan": peer},
        )

    gain = gain_ref[...]
    for b in range(batch):
        row_of = lambda way: jnp.concatenate(
            [entry[way, 4 + 2 * b + h : 5 + 2 * b + h, :] for h in range(channels // LANES)], axis=1
        )
        entering = {0: row_of(0)}
        for k in range(blocks - 1):
            entering[k + 1] = shrink[b, k] * (entering[k] + gain_up[b, k])
        leaving = {blocks - 1: shrink[b, blocks - 1] * row_of(1)}
        for k in reversed(range(blocks - 1)):
            leaving[k] = shrink[b, k] * (leaving[k + 1] + gain_down[b, k + 1])
        squares = jnp.zeros((8, LANES), F32)
        for k in range(blocks):
            for r in range(0, BLOCK, CHUNK):
                at = pl.ds(k * BLOCK + r, CHUNK)
                y = base[b, at, :] + into[b, at, :] * entering[k] + back[b, at, :] * leaving[k]
                base[b, at, :] = y * gain
                y = y * y
                y = y[:, :LANES] + y[:, LANES:]
                y = jnp.sum(y, axis=1, keepdims=True)
                y = jnp.where(lane == group + (k * BLOCK + r) // 8, y, 0.0)
                squares = squares + jnp.sum(y.reshape(CHUNK // 8, 8, LANES), axis=0)
        power[b] = squares
        for peer in c_peers:
            share(b, peer).start()

    ones = jnp.ones((2 * LANES, channels), BF16)
    lane = lax.broadcasted_iota(jnp.int32, (BLOCK, LANES), 1)
    group = lax.broadcasted_iota(jnp.int32, (BLOCK, LANES), 0) // 8
    for b in range(batch):
        squares = power[b]
        for peer in c_peers:
            shared(b, peer).wait_recv()
            squares = squares + powers[peer, b]
        scale = lax.rsqrt(squares * (1.0 / (channels * chans)) + 1e-06)
        high = scale.astype(BF16).astype(F32)
        tile = lambda a: jnp.concatenate([a] * (BLOCK // 8), axis=0)
        high, low = tile(high), tile(scale - high)
        for k in range(blocks):
            mine = lane == group + k * (BLOCK // 8)
            spread = [jnp.where(mine, a, 0.0).astype(BF16) for a in (high, low)]
            spread = dot(jnp.concatenate(spread, axis=1), ones)
            result[b, rows_of(k), :] = (base[b, rows_of(k), :] * spread).astype(BF16)
            pltpu.make_async_copy(
                result.at[b, rows_of(k), :], out_hbm.at[b, rows_of(k), :], out_sem.at[b * blocks + k]
            ).start()

    for peer in t_peers:
        told(peer).wait_send()
    for b in range(batch):
        for peer in c_peers:
            shared(b, peer).wait_send()
    for b, k in each:
        pltpu.make_async_copy(
            result.at[b, rows_of(k), :], out_hbm.at[b, rows_of(k), :], out_sem.at[b * blocks + k]
        ).wait()


def on_device(times, chans, decay_rate, drive_in, gate_in, norm_gain):
    shape = decay_rate.shape
    batch, length, channels = shape
    steps = batch * length // BLOCK
    width = 4 if times % 4 == 0 else 1
    big = lambda dtype: pltpu.VMEM(shape, dtype)
    tiles = lambda *lead: pltpu.VMEM((*lead, 8, LANES), F32)
    sems = lambda *dims: pltpu.SemaphoreType.DMA(dims)
    anywhere = pl.BlockSpec(memory_space=pl.ANY)
    return pl.pallas_call(
        functools.partial(kernel, times, chans, width),
        out_shape=jax.ShapeDtypeStruct(shape, BF16),
        in_specs=[anywhere, anywhere, anywhere, pl.BlockSpec(memory_space=pltpu.VMEM)],
        out_specs=anywhere,
        scratch_shapes=[
            big(F32), big(BF16), big(BF16),
            big(F32), big(BF16), big(BF16),
            big(F32), big(F32), big(F32), big(BF16),
            tiles(2), tiles(times), tiles(2), tiles(batch), tiles(chans, batch),
            sems(3, steps), sems(steps), sems(times), sems(times), sems(chans, batch), sems(chans, batch),
        ],
        compiler_params=pltpu.CompilerParams(
            collective_id=0, has_side_effects=True, vmem_limit_bytes=48 * 1024 * 1024
        ),
        name="two_way_scan",
    )(decay_rate, drive_in, gate_in, norm_gain.reshape(1, channels))


def solution(mesh):
    spec = P("ens", "time", "chan")
    return jax.shard_map(
        functools.partial(on_device, mesh.shape["time"], mesh.shape["chan"]),
        mesh=mesh,
        in_specs=(spec, spec, spec, P(("ens", "chan"))),
        out_specs=spec,
        check_vma=False,
    )
```

time: 367 us -> 33.6 us (0.09); the launches traced: 363 us -> 33.4 us
  blocking collectives: 156 us -> 0 us
  local copies, waits for them, and re-layouts: 161 us -> 5.69 us
  other arithmetic: 45.1 us -> 0 us
  Pallas kernels: 0 us -> 27.7 us
    all_gather x9 -> x0, blocking collectives: 156 us -> none  [the longest x8 113 us: carried_in(): pieces = jax.tree.map(lambda part: lax.all_gather(part, axis), running)]
    slice x129 -> x0, local copies, waits for them, and re-layouts: 117 us -> none  [the longest x63 63.3 us: on_device(): lax.associative_scan(join_pair, (keep, started), axis=1, reverse=True)[1]]
    pallas_call x0 -> x1, Pallas kernels: none -> 27.7 us  [on_device(): pl.pallas_call(functools.partial(kernel, times, chans, width), out_shape=...]
    pad x36 -> x0, local copies, waits for them, and re-layouts: 21.4 us -> none  [the longest x18 13.5 us: on_device(): forward = lax.associative_scan(join_pair, (keep, started), axis=1)[1]]
    rev x1 -> x0, local copies, waits for them, and re-layouts: 16.8 us -> none  [on_device(): lax.associative_scan(join_pair, (keep, started), axis=1, reverse=True)[1]]
    add x39 -> x0, other arithmetic: 13.5 us -> none  [the longest x18 5.5 us: join_pair(): return (earlier[0] * later[0], later[0] * earlier[1] + later[1])]
    mul x18 -> x0, other arithmetic: 12 us -> none  [join_pair(): return (earlier[0] * later[0], later[0] * earlier[1] + later[1])]
    reduce_sum x3 -> x0, other arithmetic: 7.78 us -> none  [the longest x1 4.32 us: on_device(): jnp.sum(gated * gated, axis=-1, keepdims=True)]
where the time goes in v1:
time: 33.6 us; the launch traced here: 33.4 us
  Pallas kernels  27.7 us (82%)
  local copies, waits for them, and re-layouts  5.69 us (17%)
    pallas_call x1, Pallas kernels, on_device(): pl.pallas_call(functools.partial(kernel, times, chans, width), out_shape=...  27.7 us
    unnamed x9, local copies, waits for them, and re-layouts  5.69 us

profile of v1, /device:TPU:1, one launch (start us, length us, event | category | flops | bytes accessed | tf_op | source)
XLA Modules:
  0.0 33.4 jit_solution(6359157715095209201)
XLA Ops:
  0.0 0.0 copy-start
  0.0 1.6 %copy-done = f32[2,1024,256]{2,1,0:T(8,128)S(1)} copy-done((f32[2,1024,256]{2,1,0:T(8,128)S(1)}, f32[2,1024,256]{2,1,0:T(8,128)}, u32[]{:S(2)}) %copy-start) | copy-done | bytes 2097176
  1.6 0.0 copy-start.1
  1.6 1.2 %copy-done.1 = bf16[2,1024,256]{2,1,0:T(8,128)(2,1)S(1)} copy-done((bf16[2,1024,256]{2,1,0:T(8,128)(2,1)S(1)}, bf16[2,1024,256]{2,1,0:T(8,128)(2,1)}, u32[]{:S(2)}) %copy-start.1) | copy-done | bytes 1048600
  2.8 0.0 copy-start.2
  2.8 1.2 %copy-done.2 = bf16[2,1024,256]{2,1,0:T(8,128)(2,1)S(1)} copy-done((bf16[2,1024,256]{2,1,0:T(8,128)(2,1)S(1)}, bf16[2,1024,256]{2,1,0:T(8,128)(2,1)}, u32[]{:S(2)}) %copy-start.2) | copy-done | bytes 1048600
  4.0 0.0 copy-start.3
  4.0 0.7 %copy-done.3 = f32[256]{0:T(256)S(1)} copy-done((f32[256]{0:T(256)S(1)}, f32[256]{0:T(256)}, u32[]{:S(2)}) %copy-start.3) | copy-done | bytes 1048
  4.7 27.7 %two_way_scan.1 = bf16[2,1024,256]{2,1,0:T(8,128)(2,1)S(1)} custom-call(f32[2,1024,256]{2,1,0:T(8,128)S(1)} %copy-done, bf16[2,1024,256]{2,1,0:T(8,128)(2,1)S(1)} %copy-done.1, bf16[2,1024,256]{2,1,0:T(8,128)(2,1)S(1)} %copy-done.2, f32[1,256]{1,0:T(1,128)S(1)} %bitcast.1), custom_call_target="tpu_custom_call" | custom-call | tf_op jit(solution)/shard_map/two_way_scan/pallas_call | solution.py:250
  32.4 1.0 %copy.6 = bf16[2,1024,256]{2,1,0:T(8,128)(2,1)} copy(bf16[2,1024,256]{2,1,0:T(8,128)(2,1)S(1)} %two_way_scan.1) | data formatting | bytes 2097152
Async XLA Ops:
  0.0 1.6 %copy-start = (f32[2,1024,256]{2,1,0:T(8,128)S(1)}, f32[2,1024,256]{2,1,0:T(8,128)}, u32[]{:S(2)}) copy-start(f32[2,1024,256]{2,1,0:T(8,128)} %decay_hbm.1) | copy-start | bytes 6291460
  1.6 1.2 %copy-start.1 = (bf16[2,1024,256]{2,1,0:T(8,128)(2,1)S(1)}, bf16[2,1024,256]{2,1,0:T(8,128)(2,1)}, u32[]{:S(2)}) copy-start(bf16[2,1024,256]{2,1,0:T(8,128)(2,1)} %drive_hbm.1) | copy-start | bytes 3145732
  2.8 1.2 %copy-start.2 = (bf16[2,1024,256]{2,1,0:T(8,128)(2,1)S(1)}, bf16[2,1024,256]{2,1,0:T(8,128)(2,1)}, u32[]{:S(2)}) copy-start(bf16[2,1024,256]{2,1,0:T(8,128)(2,1)} %gate_hbm.1) | copy-start | bytes 3145732
  4.0 0.7 %copy-start.3 = (f32[256]{0:T(256)S(1)}, f32[256]{0:T(256)}, u32[]{:S(2)}) copy-start(f32[256]{0:T(256)} %param.7) | copy-start | bytes 3076

commit v2 on v0

v2 whole, which is shorter than its diff:
```python
import functools
import math

import jax
import jax.numpy as jnp
from jax import lax
from jax.experimental import pallas as pl
from jax.experimental.pallas import tpu as pltpu
from jax.sharding import PartitionSpec as P

F32, BF16 = jnp.float32, jnp.bfloat16
BLOCK = 256
CHUNK = 32
LANES = 128


def dot(a, b):
    return lax.dot_general(a, b, (((1,), (0,)), ((), ())), preferred_element_type=F32)


def peers_by_distance(count, width):
    rows = count // width
    away = lambda s, n: min(s, n - s)
    shifts = [(r, c) for r in range(rows) for c in range(width) if r or c]
    return sorted(shifts, key=lambda s: -(away(s[0], rows) + away(s[1], width)))


def kernel(
    times, chans, width,
    decay_hbm, drive_hbm, gate_hbm, gain_hbm, result,
    decay, drive, gate, gain_ref, cum, up, down, base, into, back,
    note, notes, entry, power, powers,
    in_sem, send_sem, time_recv, chan_recv,
):
    batch, length, channels = decay.shape
    blocks, halves = length // BLOCK, channels // LANES
    each = [(b, k) for b in range(batch) for k in range(blocks)]
    rows_of = lambda k: pl.ds(k * BLOCK, BLOCK)
    chunks_of = lambda k: [pl.ds(k * BLOCK + r, CHUNK) for r in range(0, BLOCK, CHUNK)]
    fold = lambda a: jnp.sum(a.reshape(CHUNK // 8, 8, a.shape[1]), axis=0)
    total = lambda a: jnp.sum(a, axis=0, keepdims=True)
    to_power = math.log2(math.e) / (length * times)

    with jax.named_scope("start"):
        fetches = {}
        for b in range(batch):
            fetches["decay", b] = pltpu.make_async_copy(decay_hbm.at[b], decay.at[b], in_sem.at[2 * b])
            fetches["drive", b] = pltpu.make_async_copy(drive_hbm.at[b], drive.at[b], in_sem.at[2 * b + 1])
        fetches["gate"] = pltpu.make_async_copy(gate_hbm, gate, in_sem.at[2 * batch])
        fetches["gain"] = pltpu.make_async_copy(gain_hbm, gain_ref, in_sem.at[2 * batch + 1])
        for fetch in fetches.values():
            fetch.start()

    t_me, c_me = lax.axis_index("time"), lax.axis_index("chan")
    with jax.named_scope("greet"):
        tall = times // width
        shift = lambda at, by, count: jnp.where(at + by >= count, at + by - count, at + by)
        rows = [shift(t_me // width, r, tall) * width for r in range(tall)]
        columns = [shift(t_me % width, c, width) for c in range(width)]
        t_peers = [rows[r] + columns[c] for r, c in peers_by_distance(times, width)]
        c_peers = [shift(c_me, s, chans) for s in range(1, chans)]
        barrier = pltpu.get_barrier_semaphore()
        for peer in t_peers:
            pl.semaphore_signal(barrier, 1, device_id={"time": peer})
        for peer in c_peers:
            pl.semaphore_signal(barrier, 1, device_id={"chan": peer})

    iota = lambda d: lax.broadcasted_iota(jnp.int32, (BLOCK, BLOCK), d)
    lower = jnp.where(iota(0) >= iota(1), 1.0, 0.0).astype(BF16)
    upper = jnp.where(iota(0) <= iota(1), 1.0, 0.0).astype(BF16)

    shrink, gain_up, gain_down = {}, {}, {}

    def add_up(b, k):
        rising = falling = jnp.zeros((8, channels), F32)
        for at in chunks_of(k):
            logs = cum[b, at, :]
            push = drive[b, at, :].astype(F32)
            u = push * (jnp.exp2(logs * to_power) - 1.0)
            v = push * (jnp.exp2((decay[b, at, :] - logs) * to_power) - 1.0)
            up[b, at, :] = u.astype(BF16)
            down[b, at, :] = v.astype(BF16)
            rising, falling = rising + fold(u + push), falling + fold(v + push)
        shrink[b, k] = jnp.exp2(cum[b, pl.ds((k + 1) * BLOCK - 1, 1), :] * -to_power)
        gain_up[b, k] = total(rising)
        gain_down[b, k] = total(falling)

    with jax.named_scope("sums"):
        for b in range(batch):
            fetches["decay", b].wait()
            fetches["drive", b].wait()
            for k in range(blocks + 1):
                if k < blocks:
                    whole = decay[b, rows_of(k), :]
                    high = whole.astype(BF16)
                    low = (whole - high.astype(F32)).astype(BF16)
                    cum[b, rows_of(k), :] = dot(lower, high) + dot(lower, low)
                if k > 0:
                    add_up(b, k - 1)

    with jax.named_scope("summary"):
        for b in range(batch):
            kept = shrink[b, 0]
            ahead = shrink[b, 0] * gain_up[b, 0]
            for k in range(1, blocks):
                kept = kept * shrink[b, k]
                ahead = shrink[b, k] * (ahead + gain_up[b, k])
            behind = gain_down[b, blocks - 1]
            for k in reversed(range(blocks - 1)):
                behind = shrink[b, k] * behind + gain_down[b, k]
            for h in range(halves):
                lanes = slice(h * LANES, (h + 1) * LANES)
                r = b * halves + h
                for way, state in ((0, ahead), (1, behind)):
                    note[way, r : r + 1, :] = kept[:, lanes]
                    note[way, 4 + r : 5 + r, :] = state[:, lanes]

    with jax.named_scope("meet"):
        pl.semaphore_wait(barrier, len(t_peers) + len(c_peers))

    with jax.named_scope("send"):
        for peer in t_peers:
            pltpu.make_async_remote_copy(
                src_ref=note.at[jnp.where(peer > t_me, 0, 1)],
                dst_ref=notes.at[t_me],
                send_sem=send_sem.at[0],
                recv_sem=time_recv,
                device_id={"time": peer},
            ).start()
        notes[t_me] = note[0]

    with jax.named_scope("inner"):
        fetches["gate"].wait()
        for n in range(len(each) + 1):
            if n < len(each):
                b, k = each[n]
                push = drive[b, rows_of(k), :]
                base[b, rows_of(k), :] = dot(lower, push) + dot(lower, up[b, rows_of(k), :])
                into[b, rows_of(k), :] = dot(upper, push) + dot(upper, down[b, rows_of(k), :])
            if n > 0:
                b, k = each[n - 1]
                for at in chunks_of(k):
                    logs = cum[b, at, :]
                    g = gate[b, at, :].astype(F32)
                    g = g * ((length * times) ** -0.5) / (1.0 + jnp.exp(-g))
                    p = g * jnp.exp2(logs * -to_power)
                    q = g * jnp.exp2((logs - decay[b, at, :]) * to_power)
                    base[b, at, :] = p * base[b, at, :] + q * into[b, at, :]
                    into[b, at, :] = p
                    back[b, at, :] = q

    def all_of(ref, count, sem):
        return pltpu.make_async_copy(ref.at[pl.ds(0, count)], ref.at[pl.ds(0, count)], sem)

    with jax.named_scope("receive"):
        all_of(notes, times - 1, time_recv).wait()

    with jax.named_scope("fold"):
        ahead = behind = jnp.zeros((8, LANES), F32)
        for t in range(times):
            one = notes[t]
            ahead = jnp.where(t < t_me, ahead * pltpu.roll(one, 4, 0) + one, ahead)
            one = notes[times - 1 - t]
            behind = jnp.where(times - 1 - t > t_me, behind * pltpu.roll(one, 4, 0) + one, behind)
        entry[0] = ahead
        entry[1] = behind

    lane = lax.broadcasted_iota(jnp.int32, (CHUNK, LANES), 1)
    group = lax.broadcasted_iota(jnp.int32, (CHUNK, LANES), 0) // 8
    with jax.named_scope("powers"):
        for b in range(batch):
            row_of = lambda way: jnp.concatenate(
                [entry[way, 4 + halves * b + h : 5 + halves * b + h, :] for h in range(halves)], axis=1
            )
            entering = {0: row_of(0)}
            for k in range(blocks - 1):
                entering[k + 1] = shrink[b, k] * (entering[k] + gain_up[b, k])
            leaving = {blocks - 1: shrink[b, blocks - 1] * row_of(1)}
            for k in reversed(range(blocks - 1)):
                leaving[k] = shrink[b, k] * (leaving[k + 1] + gain_down[b, k + 1])
            squares = jnp.zeros((8, LANES), F32)
            for k in range(blocks):
                for r, at in enumerate(chunks_of(k)):
                    y = base[b, at, :] + into[b, at, :] * entering[k] + back[b, at, :] * leaving[k]
                    base[b, at, :] = y
                    y = y * y
                    y = jnp.sum(y[:, :LANES] + y[:, LANES:], axis=1, keepdims=True)
                    squares = squares + fold(jnp.where(lane == group + (k * BLOCK + r * CHUNK) // 8, y, 0.0))
            power[b] = squares
            for peer in c_peers:
                pltpu.make_async_remote_copy(
                    src_ref=power.at[b],
                    dst_ref=powers.at[b, c_me],
                    send_sem=send_sem.at[1],
                    recv_sem=chan_recv.at[b],
                    device_id={"chan": peer},
                ).start()

    with jax.named_scope("gain"):
        fetches["gain"].wait()
        gain = gain_ref[...]
        for b, k in each:
            for at in chunks_of(k):
                base[b, at, :] = base[b, at, :] * gain

    ones = jnp.ones((2 * LANES, channels), BF16)
    lane = lax.broadcasted_iota(jnp.int32, (BLOCK, LANES), 1)
    group = lax.broadcasted_iota(jnp.int32, (BLOCK, LANES), 0) // 8
    with jax.named_scope("finish"):
        for b in range(batch):
            all_of(powers.at[b], chans - 1, chan_recv.at[b]).wait()
            powers[b, c_me] = power[b]
            squares = powers[b, 0]
            for c in range(1, chans):
                squares = squares + powers[b, c]
            scale = lax.rsqrt(squares * (1.0 / (channels * chans)) + 1e-06)
            high = scale.astype(BF16).astype(F32)
            tile = lambda a: jnp.concatenate([a] * (BLOCK // 8), axis=0)
            high, low = tile(high), tile(scale - high)
            for k in range(blocks):
                mine = lane == group + k * (BLOCK // 8)
                spread = [jnp.where(mine, a, 0.0).astype(BF16) for a in (high, low)]
                spread = dot(jnp.concatenate(spread, axis=1), ones)
                result[b, rows_of(k), :] = (base[b, rows_of(k), :] * spread).astype(BF16)

    with jax.named_scope("drain"):
        all_of(notes, times - 1, send_sem.at[0]).wait()
        all_of(notes, batch * (chans - 1), send_sem.at[1]).wait()


def on_device(times, chans, decay_rate, drive_in, gate_in, norm_gain):
    shape = decay_rate.shape
    batch, length, channels = shape
    arrays = decay_rate, drive_in, gate_in, norm_gain.reshape(1, channels)
    width = 4 if times % 4 == 0 else 1
    big = lambda dtype: pltpu.VMEM(shape, dtype)
    tiles = lambda *lead: pltpu.VMEM((*lead, 8, LANES), F32)
    sems = lambda *dims: pltpu.SemaphoreType.DMA(dims)
    anywhere = pl.BlockSpec(memory_space=pltpu.HBM)
    return pl.pallas_call(
        functools.partial(kernel, times, chans, width),
        out_shape=jax.ShapeDtypeStruct(shape, BF16),
        in_specs=[anywhere] * 4,
        out_specs=pl.BlockSpec(memory_space=pltpu.VMEM),
        scratch_shapes=[
            big(F32), big(BF16), big(BF16), pltpu.VMEM((1, channels), F32),
            big(F32), big(BF16), big(BF16), big(F32), big(F32), big(F32),
            tiles(2), tiles(times), tiles(2), tiles(batch), tiles(batch, chans),
            sems(2 * batch + 2), sems(2), sems(), sems(batch),
        ],
        compiler_params=pltpu.CompilerParams(
            collective_id=0, has_side_effects=True, vmem_limit_bytes=48 * 1024 * 1024
        ),
        name="two_way_scan",
    )(*[pltpu.with_memory_space_constraint(a, pltpu.HBM) for a in arrays])


def solution(mesh):
    spec = P("ens", "time", "chan")
    return jax.shard_map(
        functools.partial(on_device, mesh.shape["time"], mesh.shape["chan"]),
        mesh=mesh,
        in_specs=(spec, spec, spec, P(("ens", "chan"))),
        out_specs=spec,
        check_vma=False,
    )
```

time: 367 us -> 21 us (0.06); the launches traced: 363 us -> 20.9 us
  local copies, waits for them, and re-layouts: 161 us -> 0.97 us
  blocking collectives: 156 us -> 0 us
  other arithmetic: 45.1 us -> 0 us
  Pallas kernels: 0 us -> 20 us
    all_gather x9 -> x0, blocking collectives: 156 us -> none  [the longest x8 113 us: carried_in(): pieces = jax.tree.map(lambda part: lax.all_gather(part, axis), running)]
    slice x129 -> x0, local copies, waits for them, and re-layouts: 117 us -> none  [the longest x63 63.3 us: on_device(): lax.associative_scan(join_pair, (keep, started), axis=1, reverse=True)[1]]
    pad x36 -> x0, local copies, waits for them, and re-layouts: 21.4 us -> none  [the longest x18 13.5 us: on_device(): forward = lax.associative_scan(join_pair, (keep, started), axis=1)[1]]
    pallas_call x0 -> x1, Pallas kernels: none -> 20 us  [on_device(): pl.pallas_call(functools.partial(kernel, times, chans, width), out_shape=...]
    rev x1 -> x0, local copies, waits for them, and re-layouts: 16.8 us -> none  [on_device(): lax.associative_scan(join_pair, (keep, started), axis=1, reverse=True)[1]]
    add x39 -> x0, other arithmetic: 13.5 us -> none  [the longest x18 5.5 us: join_pair(): return (earlier[0] * later[0], later[0] * earlier[1] + later[1])]
    mul x18 -> x0, other arithmetic: 12 us -> none  [join_pair(): return (earlier[0] * later[0], later[0] * earlier[1] + later[1])]
    reduce_sum x3 -> x0, other arithmetic: 7.78 us -> none  [the longest x1 4.32 us: on_device(): jnp.sum(gated * gated, axis=-1, keepdims=True)]
where the time goes in v2:
time: 21 us; the launch traced here: 20.9 us
  Pallas kernels  20 us (95%)
  local copies, waits for them, and re-layouts  0.97 us (5%)
    pallas_call x1, Pallas kernels, on_device(): pl.pallas_call(functools.partial(kernel, times, chans, width), out_shape=...  20 us
    unnamed x1, local copies, waits for them, and re-layouts  0.97 us

profile of v2, /device:TPU:1, one launch (start us, length us, event | category | flops | bytes accessed | tf_op | source)
XLA Modules:
  0.0 20.9 jit_solution(5252146370353137559)
XLA Ops:
  0.0 20.0 %two_way_scan.1 = bf16[2,1024,256]{2,1,0:T(8,128)(2,1)S(1)} custom-call(f32[2,1024,256]{2,1,0:T(8,128)} %decay_hbm.1, bf16[2,1024,256]{2,1,0:T(8,128)(2,1)} %drive_hbm.1, bf16[2,1024,256]{2,1,0:T(8,128)(2,1)} %gate_hbm.1, f32[1,256]{1,0:T(1,128)} %bitcast.1), custom_call_target="tpu_custom_call" | custom-call | tf_op jit(solution)/shard_map/two_way_scan/pallas_call | solution.py:240
  20.0 1.0 %copy.6 = bf16[2,1024,256]{2,1,0:T(8,128)(2,1)} copy(bf16[2,1024,256]{2,1,0:T(8,128)(2,1)S(1)} %two_way_scan.1) | data formatting | bytes 2097152

commit v3 on v2

--- a/solution.py
+++ b/solution.py
@@ -25,10 +25,55 @@
     return sorted(shifts, key=lambda s: -(away(s[0], rows) + away(s[1], width)))
 
 
+class Both:
+    def __init__(self, first, last):
+        self.parts = first, last
+
+    def of(self, at):
+        first, last = self.parts
+        return (last, at[1:]) if at[0] == first.shape[0] else (first, at)
+
+    def __getitem__(self, at):
+        ref, at = self.of(at)
+        return ref[at]
+
+    def __setitem__(self, at, value):
+        ref, at = self.of(at)
+        ref[at] = value
+
+
+def spread_over(scale, blocks, channels):
+    ones = jnp.ones((2 * LANES, channels), BF16)
+    lane = lax.broadcasted_iota(jnp.int32, (BLOCK, LANES), 1)
+    ahead = lane - lax.broadcasted_iota(jnp.int32, (BLOCK, LANES), 0) // 8
+    high = scale.astype(BF16).astype(F32)
+    tile = lambda a: jnp.concatenate([a] * (BLOCK // 8), axis=0)
+    parts = tile(high), tile(scale - high)
+
+    def block(k):
+        mine = ahead == k * (BLOCK // 8)
+        return dot(jnp.concatenate([jnp.where(mine, a, 0.0).astype(BF16) for a in parts], axis=1), ones)
+
+    return [functools.partial(block, k) for k in range(blocks)]
+
+
+def finish(done, last, scale, out_hbm, result, sem):
+    before, length, channels = done.shape
+    copies = [pltpu.make_async_copy(done, out_hbm.at[pl.ds(0, before)], sem.at[0])]
+    copies[0].start()
+    for k, spread in enumerate(spread_over(scale[...], length // BLOCK, channels)):
+        at = pl.ds(k * BLOCK, BLOCK)
+        result[at, :] = (last[at, :] * spread()).astype(BF16)
+        copies.append(pltpu.make_async_copy(result.at[at, :], out_hbm.at[before, at, :], sem.at[k + 1]))
+        copies[-1].start()
+    for copy in copies:
+        copy.wait()
+
+
 def kernel(
     times, chans, width,
-    decay_hbm, drive_hbm, gate_hbm, gain_hbm, result,
-    decay, drive, gate, gain_ref, cum, up, down, base, into, back,
+    decay_hbm, drive_hbm, gate_hbm, gain_hbm, done, last, last_scale,
+    decay, drive, gate, gain_ref, cum, up, down, first, into, back,
     note, notes, entry, power, powers,
     in_sem, send_sem, time_recv, chan_recv,
 ):
@@ -39,6 +84,7 @@
     chunks_of = lambda k: [pl.ds(k * BLOCK + r, CHUNK) for r in range(0, BLOCK, CHUNK)]
     fold = lambda a: jnp.sum(a.reshape(CHUNK // 8, 8, a.shape[1]), axis=0)
     total = lambda a: jnp.sum(a, axis=0, keepdims=True)
+    base = Both(first, last)
     to_power = math.log2(math.e) / (length * times)
 
     with jax.named_scope("start"):
@@ -166,7 +212,7 @@
         entry[1] = behind
 
     lane = lax.broadcasted_iota(jnp.int32, (CHUNK, LANES), 1)
-    group = lax.broadcasted_iota(jnp.int32, (CHUNK, LANES), 0) // 8
+    ahead_of = lane - lax.broadcasted_iota(jnp.int32, (CHUNK, LANES), 0) // 8
     with jax.named_scope("powers"):
         for b in range(batch):
             row_of = lambda way: jnp.concatenate(
@@ -185,7 +231,7 @@
                     base[b, at, :] = y
                     y = y * y
                     y = jnp.sum(y[:, :LANES] + y[:, LANES:], axis=1, keepdims=True)
-                    squares = squares + fold(jnp.where(lane == group + (k * BLOCK + r * CHUNK) // 8, y, 0.0))
+                    squares = squares + fold(jnp.where(ahead_of == (k * BLOCK + r * CHUNK) // 8, y, 0.0))
             power[b] = squares
             for peer in c_peers:
                 pltpu.make_async_remote_copy(
@@ -203,9 +249,6 @@
             for at in chunks_of(k):
                 base[b, at, :] = base[b, at, :] * gain
 
-    ones = jnp.ones((2 * LANES, channels), BF16)
-    lane = lax.broadcasted_iota(jnp.int32, (BLOCK, LANES), 1)
-    group = lax.broadcasted_iota(jnp.int32, (BLOCK, LANES), 0) // 8
     with jax.named_scope("finish"):
         for b in range(batch):
             all_of(powers.at[b], chans - 1, chan_recv.at[b]).wait()
@@ -214,14 +257,11 @@
             for c in range(1, chans):
                 squares = squares + powers[b, c]
             scale = lax.rsqrt(squares * (1.0 / (channels * chans)) + 1e-06)
-            high = scale.astype(BF16).astype(F32)
-            tile = lambda a: jnp.concatenate([a] * (BLOCK // 8), axis=0)
-            high, low = tile(high), tile(scale - high)
-            for k in range(blocks):
-                mine = lane == group + k * (BLOCK // 8)
-                spread = [jnp.where(mine, a, 0.0).astype(BF16) for a in (high, low)]
-                spread = dot(jnp.concatenate(spread, axis=1), ones)
-                result[b, rows_of(k), :] = (base[b, rows_of(k), :] * spread).astype(BF16)
+            if b < batch - 1:
+                for k, spread in enumerate(spread_over(scale, blocks, channels)):
+                    done[b, rows_of(k), :] = (base[b, rows_of(k), :] * spread()).astype(BF16)
+            else:
+                last_scale[...] = scale
 
     with jax.named_scope("drain"):
         all_of(notes, times - 1, send_sem.at[0]).wait()
@@ -237,14 +277,19 @@
     tiles = lambda *lead: pltpu.VMEM((*lead, 8, LANES), F32)
     sems = lambda *dims: pltpu.SemaphoreType.DMA(dims)
     anywhere = pl.BlockSpec(memory_space=pltpu.HBM)
-    return pl.pallas_call(
+    vmem = pl.BlockSpec(memory_space=pltpu.VMEM)
+    done, last, scale = pl.pallas_call(
         functools.partial(kernel, times, chans, width),
-        out_shape=jax.ShapeDtypeStruct(shape, BF16),
+        out_shape=(
+            jax.ShapeDtypeStruct((batch - 1, length, channels), BF16),
+            jax.ShapeDtypeStruct((length, channels), F32),
+            jax.ShapeDtypeStruct((8, LANES), F32),
+        ),
         in_specs=[anywhere] * 4,
-        out_specs=pl.BlockSpec(memory_space=pltpu.VMEM),
+        out_specs=(vmem, vmem, vmem),
         scratch_shapes=[
             big(F32), big(BF16), big(BF16), pltpu.VMEM((1, channels), F32),
-            big(F32), big(BF16), big(BF16), big(F32), big(F32), big(F32),
+            big(F32), big(BF16), big(BF16), pltpu.VMEM((batch - 1, length, channels), F32), big(F32), big(F32),
             tiles(2), tiles(times), tiles(2), tiles(batch), tiles(batch, chans),
             sems(2 * batch + 2), sems(2), sems(), sems(batch),
         ],
@@ -253,6 +298,15 @@
         ),
         name="two_way_scan",
     )(*[pltpu.with_memory_space_constraint(a, pltpu.HBM) for a in arrays])
+    return pl.pallas_call(
+        finish,
+        out_shape=jax.ShapeDtypeStruct(shape, BF16),
+        in_specs=[vmem, vmem, vmem],
+        out_specs=anywhere,
+        scratch_shapes=[pltpu.VMEM((length, channels), BF16), sems(length // BLOCK + 1)],
+        compiler_params=pltpu.CompilerParams(vmem_limit_bytes=8 * 1024 * 1024),
+        name="finish",
+    )(done, last, scale)
 
 
 def solution(mesh):

time: 21 us -> 20.8 us (level)
  local copies, waits for them, and re-layouts: 0.97 us -> 0 us
  Pallas kernels: 20 us -> 20.7 us
    pallas_call x0 -> x1, Pallas kernels: none -> 1.06 us  [on_device(): pl.pallas_call(finish, out_shape=jax.ShapeDtypeStruct(shape, BF16), in_sp...]
    unnamed x1 -> x0, local copies, waits for them, and re-layouts: 0.97 us -> none
    pallas_call x1, Pallas kernels: 20 us -> 19.6 us  [on_device(): pl.pallas_call(functools.partial(kernel, times, chans, width), out_shape=...]
where the time goes in v3:
time: 20.8 us; the launch traced here: 20.7 us
  Pallas kernels  20.7 us (100%)
    pallas_call x1, Pallas kernels, on_device(): pl.pallas_call(functools.partial(kernel, times, chans, width), out_shape=...  19.6 us
    pallas_call x1, Pallas kernels, on_device(): pl.pallas_call(finish, out_shape=jax.ShapeDtypeStruct(shape, BF16), in_sp...  1.06 us

profile of v3, /device:TPU:1, one launch (start us, length us, event | category | flops | bytes accessed | tf_op | source)
XLA Modules:
  0.0 20.7 jit_solution(9220179278588580023)
XLA Ops:
  0.0 19.6 %two_way_scan.1 = (bf16[1,1024,256]{2,1,0:T(8,128)(2,1)S(1)}, f32[1024,256]{1,0:T(8,128)S(1)}, f32[8,128]{1,0:T(8,128)S(1)}) custom-call(f32[2,1024,256]{2,1,0:T(8,128)} %decay_hbm.1, bf16[2,1024,256]{2,1,0:T(8,128)(2,1)} %drive_hbm.1, bf16[2,1024,256]{2,1,0:T(8,128)(2,1)} %gate_hbm.1, f32[1,256]{1,0:T(1,128)} %bitcast.1), custom_call_target="tpu_custom_call" | custom-call | tf_op jit(solution)/shard_map/two_way_scan/pallas_call | solution.py:281
  19.6 1.1 %finish.1 = bf16[2,1024,256]{2,1,0:T(8,128)(2,1)} custom-call(bf16[1,1024,256]{2,1,0:T(8,128)(2,1)S(1)} %get-tuple-element.8.done, f32[1024,256]{1,0:T(8,128)S(1)} %get-tuple-element.9.last, f32[8,128]{1,0:T(8,128)S(1)} %get-tuple-element.10.scale), custom_call_target="tpu_custom_call" | custom-call | tf_op jit(solution)/shard_map/finish/pallas_call | solution.py:301

commit v4 on v3

--- a/solution.py
+++ b/solution.py
@@ -165,7 +165,10 @@
         pl.semaphore_wait(barrier, len(t_peers) + len(c_peers))
 
     with jax.named_scope("send"):
-        for peer in t_peers:
+        instead = t_peers[0]
+        ordered = [jnp.where(t_me == 0, instead, 0)]
+        ordered += [jnp.where(peer == 0, instead, peer) for peer in t_peers[1:]]
+        for peer in ordered:
             pltpu.make_async_remote_copy(
                 src_ref=note.at[jnp.where(peer > t_me, 0, 1)],
                 dst_ref=notes.at[t_me],

time: 20.8 us -> 20.5 us (0.986)
  Pallas kernels: 20.7 us -> 20.4 us
    pallas_call x1, Pallas kernels: 19.6 us -> 19.4 us  [on_device(): pl.pallas_call(functools.partial(kernel, times, chans, width), out_shape=...]
where the time goes in v4:
time: 20.5 us
  Pallas kernels  20.4 us (100%)
    pallas_call x1, Pallas kernels, on_device(): pl.pallas_call(functools.partial(kernel, times, chans, width), out_shape=...  19.4 us
    pallas_call x1, Pallas kernels, on_device(): pl.pallas_call(finish, out_shape=jax.ShapeDtypeStruct(shape, BF16), in_sp...  1.06 us

profile of v4, /device:TPU:1, one launch (start us, length us, event | category | flops | bytes accessed | tf_op | source)
XLA Modules:
  0.0 20.5 jit_solution(11870817064596445396)
XLA Ops:
  0.0 19.4 %two_way_scan.1 = (bf16[1,1024,256]{2,1,0:T(8,128)(2,1)S(1)}, f32[1024,256]{1,0:T(8,128)S(1)}, f32[8,128]{1,0:T(8,128)S(1)}) custom-call(f32[2,1024,256]{2,1,0:T(8,128)} %decay_hbm.1, bf16[2,1024,256]{2,1,0:T(8,128)(2,1)} %drive_hbm.1, bf16[2,1024,256]{2,1,0:T(8,128)(2,1)} %gate_hbm.1, f32[1,256]{1,0:T(1,128)} %bitcast.1), custom_call_target="tpu_custom_call" | custom-call | tf_op jit(solution)/shard_map/two_way_scan/pallas_call | solution.py:284
  19.4 1.1 %finish.1 = bf16[2,1024,256]{2,1,0:T(8,128)(2,1)} custom-call(bf16[1,1024,256]{2,1,0:T(8,128)(2,1)S(1)} %get-tuple-element.8.done, f32[1024,256]{1,0:T(8,128)S(1)} %get-tuple-element.9.last, f32[8,128]{1,0:T(8,128)S(1)} %get-tuple-element.10.scale), custom_call_target="tpu_custom_call" | custom-call | tf_op jit(solution)/shard_map/finish/pallas_call | solution.py:304

commit v5 on v4

--- a/solution.py
+++ b/solution.py
@@ -118,18 +118,19 @@
     shrink, gain_up, gain_down = {}, {}, {}
 
     def add_up(b, k):
-        rising = falling = jnp.zeros((8, channels), F32)
+        whole = plain = rising = falling = jnp.zeros((8, channels), F32)
         for at in chunks_of(k):
-            logs = cum[b, at, :]
+            logs, step = cum[b, at, :], decay[b, at, :]
             push = drive[b, at, :].astype(F32)
             u = push * (jnp.exp2(logs * to_power) - 1.0)
-            v = push * (jnp.exp2((decay[b, at, :] - logs) * to_power) - 1.0)
+            v = push * (jnp.exp2((step - logs) * to_power) - 1.0)
             up[b, at, :] = u.astype(BF16)
             down[b, at, :] = v.astype(BF16)
-            rising, falling = rising + fold(u + push), falling + fold(v + push)
-        shrink[b, k] = jnp.exp2(cum[b, pl.ds((k + 1) * BLOCK - 1, 1), :] * -to_power)
-        gain_up[b, k] = total(rising)
-        gain_down[b, k] = total(falling)
+            whole, plain = whole + fold(step), plain + fold(push)
+            rising, falling = rising + fold(u), falling + fold(v)
+        shrink[b, k] = jnp.exp2(total(whole) * -to_power)
+        gain_up[b, k] = total(plain + rising)
+        gain_down[b, k] = total(plain + falling)
 
     with jax.named_scope("sums"):
         for b in range(batch):
@@ -137,10 +138,7 @@
             fetches["drive", b].wait()
             for k in range(blocks + 1):
                 if k < blocks:
-                    whole = decay[b, rows_of(k), :]
-                    high = whole.astype(BF16)
-                    low = (whole - high.astype(F32)).astype(BF16)
-                    cum[b, rows_of(k), :] = dot(lower, high) + dot(lower, low)
+                    cum[b, rows_of(k), :] = dot(lower, decay[b, rows_of(k), :].astype(BF16))
                 if k > 0:
                     add_up(b, k - 1)
 

time: 20.5 us -> 20.2 us (0.985)
  Pallas kernels: 20.4 us -> 20.1 us
    pallas_call x1, Pallas kernels: 19.4 us -> 19.1 us  [on_device(): pl.pallas_call(functools.partial(kernel, times, chans, width), out_shape=...]
where the time goes in v5:
time: 20.2 us; the launch traced here: 20.1 us
  Pallas kernels  20.1 us (100%)
    pallas_call x1, Pallas kernels, on_device(): pl.pallas_call(functools.partial(kernel, times, chans, width), out_shape=...  19.1 us
    pallas_call x1, Pallas kernels, on_device(): pl.pallas_call(finish, out_shape=jax.ShapeDtypeStruct(shape, BF16), in_sp...  1.06 us

profile of v5, /device:TPU:1, one launch (start us, length us, event | category | flops | bytes accessed | tf_op | source)
XLA Modules:
  0.0 20.1 jit_solution(15906298018857806898)
XLA Ops:
  0.0 19.1 %two_way_scan.1 = (bf16[1,1024,256]{2,1,0:T(8,128)(2,1)S(1)}, f32[1024,256]{1,0:T(8,128)S(1)}, f32[8,128]{1,0:T(8,128)S(1)}) custom-call(f32[2,1024,256]{2,1,0:T(8,128)} %decay_hbm.1, bf16[2,1024,256]{2,1,0:T(8,128)(2,1)} %drive_hbm.1, bf16[2,1024,256]{2,1,0:T(8,128)(2,1)} %gate_hbm.1, f32[1,256]{1,0:T(1,128)} %bitcast.1), custom_call_target="tpu_custom_call" | custom-call | tf_op jit(solution)/shard_map/two_way_scan/pallas_call | solution.py:282
  19.1 1.1 %finish.1 = bf16[2,1024,256]{2,1,0:T(8,128)(2,1)} custom-call(bf16[1,1024,256]{2,1,0:T(8,128)(2,1)S(1)} %get-tuple-element.8.done, f32[1024,256]{1,0:T(8,128)S(1)} %get-tuple-element.9.last, f32[8,128]{1,0:T(8,128)S(1)} %get-tuple-element.10.scale), custom_call_target="tpu_custom_call" | custom-call | tf_op jit(solution)/shard_map/finish/pallas_call | solution.py:302

commit v6 on v5

--- a/solution.py
+++ b/solution.py
@@ -42,28 +42,34 @@
         ref[at] = value
 
 
-def spread_over(scale, blocks, channels):
-    ones = jnp.ones((2 * LANES, channels), BF16)
-    lane = lax.broadcasted_iota(jnp.int32, (BLOCK, LANES), 1)
-    ahead = lane - lax.broadcasted_iota(jnp.int32, (BLOCK, LANES), 0) // 8
+def spreader(scale):
+    iota = lambda d, shape: lax.broadcasted_iota(jnp.int32, shape, d)
+    square = (2 * LANES, 2 * LANES)
+    ones = jnp.where((iota(0, square) % 32 < 16) == (iota(1, square) < LANES), 1.0, 0.0).astype(BF16)
+    lane = iota(1, (BLOCK // 2, LANES))
+    ahead = lane % 16 + lane // 32 * 16 - iota(0, (BLOCK // 2, LANES)) // 8
     high = scale.astype(BF16).astype(F32)
-    tile = lambda a: jnp.concatenate([a] * (BLOCK // 8), axis=0)
+    tile = lambda a: jnp.concatenate([a] * (BLOCK // 16), axis=0)
     parts = tile(high), tile(scale - high)
 
     def block(k):
-        mine = ahead == k * (BLOCK // 8)
-        return dot(jnp.concatenate([jnp.where(mine, a, 0.0).astype(BF16) for a in parts], axis=1), ones)
-
-    return [functools.partial(block, k) for k in range(blocks)]
+        mine = ahead == k * 16
+        both = dot(jnp.concatenate([jnp.where(mine, a, 0.0).astype(BF16) for a in parts], axis=1), ones)
+        return [jnp.concatenate([half, half], axis=1) for half in (both[:, :LANES], both[:, LANES:])]
+
+    return block
 
 
 def finish(done, last, scale, out_hbm, result, sem):
     before, length, channels = done.shape
     copies = [pltpu.make_async_copy(done, out_hbm.at[pl.ds(0, before)], sem.at[0])]
     copies[0].start()
-    for k, spread in enumerate(spread_over(scale[...], length // BLOCK, channels)):
+    spread_over = spreader(scale[...])
+    for k in range(length // BLOCK):
+        for h, spread in enumerate(spread_over(k)):
+            at = pl.ds(k * BLOCK + h * BLOCK // 2, BLOCK // 2)
+            result[at, :] = (last[at, :] * spread).astype(BF16)
         at = pl.ds(k * BLOCK, BLOCK)
-        result[at, :] = (last[at, :] * spread()).astype(BF16)
         copies.append(pltpu.make_async_copy(result.at[at, :], out_hbm.at[before, at, :], sem.at[k + 1]))
         copies[-1].start()
     for copy in copies:
@@ -212,8 +218,6 @@
         entry[0] = ahead
         entry[1] = behind
 
-    lane = lax.broadcasted_iota(jnp.int32, (CHUNK, LANES), 1)
-    ahead_of = lane - lax.broadcasted_iota(jnp.int32, (CHUNK, LANES), 0) // 8
     with jax.named_scope("powers"):
         for b in range(batch):
             row_of = lambda way: jnp.concatenate(
@@ -225,15 +229,15 @@
             leaving = {blocks - 1: shrink[b, blocks - 1] * row_of(1)}
             for k in reversed(range(blocks - 1)):
                 leaving[k] = shrink[b, k] * (leaving[k + 1] + gain_down[b, k + 1])
-            squares = jnp.zeros((8, LANES), F32)
             for k in range(blocks):
                 for r, at in enumerate(chunks_of(k)):
                     y = base[b, at, :] + into[b, at, :] * entering[k] + back[b, at, :] * leaving[k]
                     base[b, at, :] = y
                     y = y * y
                     y = jnp.sum(y[:, :LANES] + y[:, LANES:], axis=1, keepdims=True)
-                    squares = squares + fold(jnp.where(ahead_of == (k * BLOCK + r * CHUNK) // 8, y, 0.0))
-            power[b] = squares
+                    for g in range(CHUNK // 8):
+                        q = (k * BLOCK + r * CHUNK) // 8 + g
+                        power[b, :, q : q + 1] = y[8 * g : 8 * g + 8]
             for peer in c_peers:
                 pltpu.make_async_remote_copy(
                     src_ref=power.at[b],
@@ -259,8 +263,11 @@
                 squares = squares + powers[b, c]
             scale = lax.rsqrt(squares * (1.0 / (channels * chans)) + 1e-06)
             if b < batch - 1:
-                for k, spread in enumerate(spread_over(scale, blocks, channels)):
-                    done[b, rows_of(k), :] = (base[b, rows_of(k), :] * spread()).astype(BF16)
+                spread_over = spreader(scale)
+                for k in range(blocks):
+                    for h, spread in enumerate(spread_over(k)):
+                        at = pl.ds(k * BLOCK + h * BLOCK // 2, BLOCK // 2)
+                        done[b, at, :] = (base[b, at, :] * spread).astype(BF16)
             else:
                 last_scale[...] = scale
 

time: 20.2 us -> 20.1 us (level)
  no operation moved by 1% of the time
where the time goes in v6:
time: 20.1 us
  Pallas kernels  20.1 us (100%)
    pallas_call x1, Pallas kernels, on_device(): pl.pallas_call(functools.partial(kernel, times, chans, width), out_shape=...  19 us
    pallas_call x1, Pallas kernels, on_device(): pl.pallas_call(finish, out_shape=jax.ShapeDtypeStruct(shape, BF16), in_sp...  1.03 us

profile of v6, /device:TPU:1, one launch (start us, length us, event | category | flops | bytes accessed | tf_op | source)
XLA Modules:
  0.0 20.1 jit_solution(2665246631643856334)
XLA Ops:
  0.0 19.0 %two_way_scan.1 = (bf16[1,1024,256]{2,1,0:T(8,128)(2,1)S(1)}, f32[1024,256]{1,0:T(8,128)S(1)}, f32[8,128]{1,0:T(8,128)S(1)}) custom-call(f32[2,1024,256]{2,1,0:T(8,128)} %decay_hbm.1, bf16[2,1024,256]{2,1,0:T(8,128)(2,1)} %drive_hbm.1, bf16[2,1024,256]{2,1,0:T(8,128)(2,1)} %gate_hbm.1, f32[1,256]{1,0:T(1,128)} %bitcast.1), custom_call_target="tpu_custom_call" | custom-call | tf_op jit(solution)/shard_map/two_way_scan/pallas_call | solution.py:289
  19.0 1.0 %finish.1 = bf16[2,1024,256]{2,1,0:T(8,128)(2,1)} custom-call(bf16[1,1024,256]{2,1,0:T(8,128)(2,1)S(1)} %get-tuple-element.8.done, f32[1024,256]{1,0:T(8,128)S(1)} %get-tuple-element.9.last, f32[8,128]{1,0:T(8,128)S(1)} %get-tuple-element.10.scale), custom_call_target="tpu_custom_call" | custom-call | tf_op jit(solution)/shard_map/finish/pallas_call | solution.py:309

commit v7 on v6

--- a/solution.py
+++ b/solution.py
@@ -110,7 +110,7 @@
         rows = [shift(t_me // width, r, tall) * width for r in range(tall)]
         columns = [shift(t_me % width, c, width) for c in range(width)]
         t_peers = [rows[r] + columns[c] for r, c in peers_by_distance(times, width)]
-        c_peers = [shift(c_me, s, chans) for s in range(1, chans)]
+        c_peers = [shift(c_me, s, chans) for s in reversed(range(1, chans))]
         barrier = pltpu.get_barrier_semaphore()
         for peer in t_peers:
             pl.semaphore_signal(barrier, 1, device_id={"time": peer})

time: 20.1 us -> 19.9 us (0.990)
  Pallas kernels: 20.1 us -> 19.8 us
    pallas_call x1, Pallas kernels: 19 us -> 18.8 us  [on_device(): pl.pallas_call(functools.partial(kernel, times, chans, width), out_shape=...]
where the time goes in v7:
time: 19.9 us; the launch traced here: 19.8 us
  Pallas kernels  19.8 us (99%)
    pallas_call x1, Pallas kernels, on_device(): pl.pallas_call(functools.partial(kernel, times, chans, width), out_shape=...  18.8 us
    pallas_call x1, Pallas kernels, on_device(): pl.pallas_call(finish, out_shape=jax.ShapeDtypeStruct(shape, BF16), in_sp...  1.03 us

profile of v7, /device:TPU:1, one launch (start us, length us, event | category | flops | bytes accessed | tf_op | source)
XLA Modules:
  0.0 19.8 jit_solution(16837230716625518243)
XLA Ops:
  0.0 18.8 %two_way_scan.1 = (bf16[1,1024,256]{2,1,0:T(8,128)(2,1)S(1)}, f32[1024,256]{1,0:T(8,128)S(1)}, f32[8,128]{1,0:T(8,128)S(1)}) custom-call(f32[2,1024,256]{2,1,0:T(8,128)} %decay_hbm.1, bf16[2,1024,256]{2,1,0:T(8,128)(2,1)} %drive_hbm.1, bf16[2,1024,256]{2,1,0:T(8,128)(2,1)} %gate_hbm.1, f32[1,256]{1,0:T(1,128)} %bitcast.1), custom_call_target="tpu_custom_call" | custom-call | tf_op jit(solution)/shard_map/two_way_scan/pallas_call | solution.py:289
  18.8 1.0 %finish.1 = bf16[2,1024,256]{2,1,0:T(8,128)(2,1)} custom-call(bf16[1,1024,256]{2,1,0:T(8,128)(2,1)S(1)} %get-tuple-element.8.done, f32[1024,256]{1,0:T(8,128)S(1)} %get-tuple-element.9.last, f32[8,128]{1,0:T(8,128)S(1)} %get-tuple-element.10.scale), custom_call_target="tpu_custom_call" | custom-call | tf_op jit(solution)/shard_map/finish/pallas_call | solution.py:309

commit v8 on v7

--- a/solution.py
+++ b/solution.py
@@ -43,21 +43,13 @@
 
 
 def spreader(scale):
-    iota = lambda d, shape: lax.broadcasted_iota(jnp.int32, shape, d)
-    square = (2 * LANES, 2 * LANES)
-    ones = jnp.where((iota(0, square) % 32 < 16) == (iota(1, square) < LANES), 1.0, 0.0).astype(BF16)
-    lane = iota(1, (BLOCK // 2, LANES))
-    ahead = lane % 16 + lane // 32 * 16 - iota(0, (BLOCK // 2, LANES)) // 8
-    high = scale.astype(BF16).astype(F32)
-    tile = lambda a: jnp.concatenate([a] * (BLOCK // 16), axis=0)
-    parts = tile(high), tile(scale - high)
-
-    def block(k):
-        mine = ahead == k * 16
-        both = dot(jnp.concatenate([jnp.where(mine, a, 0.0).astype(BF16) for a in parts], axis=1), ones)
-        return [jnp.concatenate([half, half], axis=1) for half in (both[:, :LANES], both[:, LANES:])]
-
-    return block
+    def half(first):
+        lanes = range(first, first + BLOCK // 16)
+        rows = [jnp.broadcast_to(scale[:, q : q + 1], scale.shape) for q in lanes]
+        both = jnp.concatenate(rows, axis=0)
+        return jnp.concatenate([both, both], axis=1)
+
+    return lambda k: [half((2 * k + h) * BLOCK // 16) for h in range(2)]
 
 
 def finish(done, last, scale, out_hbm, result, sem):

time: 19.9 us -> 19.9 us (level)
  no operation moved by 1% of the time
where the time goes in v8:
time: 19.9 us; the launch traced here: 19.8 us
  Pallas kernels  19.8 us (99%)
    pallas_call x1, Pallas kernels, on_device(): pl.pallas_call(functools.partial(kernel, times, chans, width), out_shape=...  18.8 us
    pallas_call x1, Pallas kernels, on_device(): pl.pallas_call(finish, out_shape=jax.ShapeDtypeStruct(shape, BF16), in_sp...  1 us

profile of v8, /device:TPU:1, one launch (start us, length us, event | category | flops | bytes accessed | tf_op | source)
XLA Modules:
  0.0 19.8 jit_solution(8628631254198521711)
XLA Ops:
  0.0 18.8 %two_way_scan.1 = (bf16[1,1024,256]{2,1,0:T(8,128)(2,1)S(1)}, f32[1024,256]{1,0:T(8,128)S(1)}, f32[8,128]{1,0:T(8,128)S(1)}) custom-call(f32[2,1024,256]{2,1,0:T(8,128)} %decay_hbm.1, bf16[2,1024,256]{2,1,0:T(8,128)(2,1)} %drive_hbm.1, bf16[2,1024,256]{2,1,0:T(8,128)(2,1)} %gate_hbm.1, f32[1,256]{1,0:T(1,128)} %bitcast.1), custom_call_target="tpu_custom_call" | custom-call | tf_op jit(solution)/shard_map/two_way_scan/pallas_call | solution.py:281
  18.8 1.0 %finish.1 = bf16[2,1024,256]{2,1,0:T(8,128)(2,1)} custom-call(bf16[1,1024,256]{2,1,0:T(8,128)(2,1)S(1)} %get-tuple-element.8.done, f32[1024,256]{1,0:T(8,128)S(1)} %get-tuple-element.9.last, f32[8,128]{1,0:T(8,128)S(1)} %get-tuple-element.10.scale), custom_call_target="tpu_custom_call" | custom-call | tf_op jit(solution)/shard_map/finish/pallas_call | solution.py:301

commit v9 on v8

--- a/solution.py
+++ b/solution.py
@@ -54,18 +54,15 @@
 
 def finish(done, last, scale, out_hbm, result, sem):
     before, length, channels = done.shape
-    copies = [pltpu.make_async_copy(done, out_hbm.at[pl.ds(0, before)], sem.at[0])]
-    copies[0].start()
+    pltpu.make_async_copy(done, out_hbm.at[pl.ds(0, before)], sem).start()
     spread_over = spreader(scale[...])
     for k in range(length // BLOCK):
         for h, spread in enumerate(spread_over(k)):
             at = pl.ds(k * BLOCK + h * BLOCK // 2, BLOCK // 2)
             result[at, :] = (last[at, :] * spread).astype(BF16)
         at = pl.ds(k * BLOCK, BLOCK)
-        copies.append(pltpu.make_async_copy(result.at[at, :], out_hbm.at[before, at, :], sem.at[k + 1]))
-        copies[-1].start()
-    for copy in copies:
-        copy.wait()
+        pltpu.make_async_copy(result.at[at, :], out_hbm.at[before, at, :], sem).start()
+    pltpu.make_async_copy(out_hbm, out_hbm, sem).wait()
 
 
 def kernel(
@@ -303,7 +300,7 @@
         out_shape=jax.ShapeDtypeStruct(shape, BF16),
         in_specs=[vmem, vmem, vmem],
         out_specs=anywhere,
-        scratch_shapes=[pltpu.VMEM((length, channels), BF16), sems(length // BLOCK + 1)],
+        scratch_shapes=[pltpu.VMEM((length, channels), BF16), sems()],
         compiler_params=pltpu.CompilerParams(vmem_limit_bytes=8 * 1024 * 1024),
         name="finish",
     )(done, last, scale)

time: 19.9 us -> 19.8 us (level)
  no operation moved by 1% of the time
where the time goes in v9:
time: 19.8 us
  Pallas kernels  19.8 us (100%)
    pallas_call x1, Pallas kernels, on_device(): pl.pallas_call(functools.partial(kernel, times, chans, width), out_shape=...  18.8 us
    pallas_call x1, Pallas kernels, on_device(): pl.pallas_call(finish, out_shape=jax.ShapeDtypeStruct(shape, BF16), in_sp...  0.97 us

profile of v9, /device:TPU:1, one launch (start us, length us, event | category | flops | bytes accessed | tf_op | source)
XLA Modules:
  0.0 19.8 jit_solution(13989230117976103917)
XLA Ops:
  0.0 18.8 %two_way_scan.1 = (bf16[1,1024,256]{2,1,0:T(8,128)(2,1)S(1)}, f32[1024,256]{1,0:T(8,128)S(1)}, f32[8,128]{1,0:T(8,128)S(1)}) custom-call(f32[2,1024,256]{2,1,0:T(8,128)} %decay_hbm.1, bf16[2,1024,256]{2,1,0:T(8,128)(2,1)} %drive_hbm.1, bf16[2,1024,256]{2,1,0:T(8,128)(2,1)} %gate_hbm.1, f32[1,256]{1,0:T(1,128)} %bitcast.1), custom_call_target="tpu_custom_call" | custom-call | tf_op jit(solution)/shard_map/two_way_scan/pallas_call | solution.py:278
  18.8 1.0 %finish.1 = bf16[2,1024,256]{2,1,0:T(8,128)(2,1)} custom-call(bf16[1,1024,256]{2,1,0:T(8,128)(2,1)S(1)} %get-tuple-element.8.done, f32[1024,256]{1,0:T(8,128)S(1)} %get-tuple-element.9.last, f32[8,128]{1,0:T(8,128)S(1)} %get-tuple-element.10.scale), custom_call_target="tpu_custom_call" | custom-call | tf_op jit(solution)/shard_map/finish/pallas_call | solution.py:298

commit v10 on v9

--- a/solution.py
+++ b/solution.py
@@ -85,10 +85,10 @@
     with jax.named_scope("start"):
         fetches = {}
         for b in range(batch):
-            fetches["decay", b] = pltpu.make_async_copy(decay_hbm.at[b], decay.at[b], in_sem.at[2 * b])
-            fetches["drive", b] = pltpu.make_async_copy(drive_hbm.at[b], drive.at[b], in_sem.at[2 * b + 1])
-        fetches["gate"] = pltpu.make_async_copy(gate_hbm, gate, in_sem.at[2 * batch])
-        fetches["gain"] = pltpu.make_async_copy(gain_hbm, gain_ref, in_sem.at[2 * batch + 1])
+            fetches["decay", b] = pltpu.make_async_copy(decay_hbm.at[b], decay.at[b], in_sem.at[b])
+            fetches["drive", b] = pltpu.make_async_copy(drive_hbm.at[b], drive.at[b], in_sem.at[b])
+        fetches["gate"] = pltpu.make_async_copy(gate_hbm, gate, in_sem.at[batch])
+        fetches["gain"] = pltpu.make_async_copy(gain_hbm, gain_ref, in_sem.at[batch + 1])
         for fetch in fetches.values():
             fetch.start()
 
@@ -129,8 +129,8 @@
 
     with jax.named_scope("sums"):
         for b in range(batch):
-            fetches["decay", b].wait()
-            fetches["drive", b].wait()
+            both = decay.at[pl.ds(0, 2), pl.ds(0, length * 3 // 4), :]
+            pltpu.make_async_copy(both, both, in_sem.at[b]).wait()
             for k in range(blocks + 1):
                 if k < blocks:
                     cum[b, rows_of(k), :] = dot(lower, decay[b, rows_of(k), :].astype(BF16))
@@ -288,7 +288,7 @@
             big(F32), big(BF16), big(BF16), pltpu.VMEM((1, channels), F32),
             big(F32), big(BF16), big(BF16), pltpu.VMEM((batch - 1, length, channels), F32), big(F32), big(F32),
             tiles(2), tiles(times), tiles(2), tiles(batch), tiles(batch, chans),
-            sems(2 * batch + 2), sems(2), sems(), sems(batch),
+            sems(batch + 2), sems(2), sems(), sems(batch),
         ],
         compiler_params=pltpu.CompilerParams(
             collective_id=0, has_side_effects=True, vmem_limit_bytes=48 * 1024 * 1024

time: 19.8 us -> 19.8 us (level)
  no operation moved by 1% of the time
where the time goes in v10:
time: 19.8 us; the launch traced here: 19.7 us
  Pallas kernels  19.7 us (99%)
    pallas_call x1, Pallas kernels, on_device(): pl.pallas_call(functools.partial(kernel, times, chans, width), out_shape=...  18.8 us
    pallas_call x1, Pallas kernels, on_device(): pl.pallas_call(finish, out_shape=jax.ShapeDtypeStruct(shape, BF16), in_sp...  0.97 us

profile of v10, /device:TPU:1, one launch (start us, length us, event | category | flops | bytes accessed | tf_op | source)
XLA Modules:
  0.0 19.7 jit_solution(15483375827434300699)
XLA Ops:
  0.0 18.8 %two_way_scan.1 = (bf16[1,1024,256]{2,1,0:T(8,128)(2,1)S(1)}, f32[1024,256]{1,0:T(8,128)S(1)}, f32[8,128]{1,0:T(8,128)S(1)}) custom-call(f32[2,1024,256]{2,1,0:T(8,128)} %decay_hbm.1, bf16[2,1024,256]{2,1,0:T(8,128)(2,1)} %drive_hbm.1, bf16[2,1024,256]{2,1,0:T(8,128)(2,1)} %gate_hbm.1, f32[1,256]{1,0:T(1,128)} %bitcast.1), custom_call_target="tpu_custom_call" | custom-call | tf_op jit(solution)/shard_map/two_way_scan/pallas_call | solution.py:278
  18.8 1.0 %finish.1 = bf16[2,1024,256]{2,1,0:T(8,128)(2,1)} custom-call(bf16[1,1024,256]{2,1,0:T(8,128)(2,1)S(1)} %get-tuple-element.8.done, f32[1024,256]{1,0:T(8,128)S(1)} %get-tuple-element.9.last, f32[8,128]{1,0:T(8,128)S(1)} %get-tuple-element.10.scale), custom_call_target="tpu_custom_call" | custom-call | tf_op jit(solution)/shard_map/finish/pallas_call | solution.py:298

commit v11 on v10

--- a/solution.py
+++ b/solution.py
@@ -198,12 +198,23 @@
         all_of(notes, times - 1, time_recv).wait()
 
     with jax.named_scope("fold"):
-        ahead = behind = jnp.zeros((8, LANES), F32)
-        for t in range(times):
-            one = notes[t]
-            ahead = jnp.where(t < t_me, ahead * pltpu.roll(one, 4, 0) + one, ahead)
-            one = notes[times - 1 - t]
-            behind = jnp.where(times - 1 - t > t_me, behind * pltpu.roll(one, 4, 0) + one, behind)
+        nothing = jnp.where(lax.broadcasted_iota(jnp.int32, (8, LANES), 0) < 4, 1.0, 0.0)
+
+        def chain(ts, counts):
+            kept = state = None
+            for t in ts:
+                one = jnp.where(counts(t), notes[t], nothing)
+                keep = pltpu.roll(one, 4, 0)
+                kept, state = (keep, one) if state is None else (kept * keep, state * keep + one)
+            return kept, state
+
+        def both(ts, counts):
+            _, state = chain(ts[: len(ts) // 2], counts)
+            kept, more = chain(ts[len(ts) // 2 :], counts)
+            return state * kept + more
+
+        ahead = both(list(range(times)), lambda t: t < t_me)
+        behind = both(list(reversed(range(times))), lambda t: t > t_me)
         entry[0] = ahead
         entry[1] = behind
 

time: 19.8 us -> 19.8 us (level)
  no operation moved by 1% of the time
where the time goes in v11:
time: 19.8 us; the launch traced here: 19.7 us
  Pallas kernels  19.7 us (99%)
    pallas_call x1, Pallas kernels, on_device(): pl.pallas_call(functools.partial(kernel, times, chans, width), out_shape=...  18.8 us
    pallas_call x1, Pallas kernels, on_device(): pl.pallas_call(finish, out_shape=jax.ShapeDtypeStruct(shape, BF16), in_sp...  0.97 us

profile of v11, /device:TPU:1, one launch (start us, length us, event | category | flops | bytes accessed | tf_op | source)
XLA Modules:
  0.0 19.7 jit_solution(3154100575902297727)
XLA Ops:
  0.0 18.8 %two_way_scan.1 = (bf16[1,1024,256]{2,1,0:T(8,128)(2,1)S(1)}, f32[1024,256]{1,0:T(8,128)S(1)}, f32[8,128]{1,0:T(8,128)S(1)}) custom-call(f32[2,1024,256]{2,1,0:T(8,128)} %decay_hbm.1, bf16[2,1024,256]{2,1,0:T(8,128)(2,1)} %drive_hbm.1, bf16[2,1024,256]{2,1,0:T(8,128)(2,1)} %gate_hbm.1, f32[1,256]{1,0:T(1,128)} %bitcast.1), custom_call_target="tpu_custom_call" | custom-call | tf_op jit(solution)/shard_map/two_way_scan/pallas_call | solution.py:289
  18.8 1.0 %finish.1 = bf16[2,1024,256]{2,1,0:T(8,128)(2,1)} custom-call(bf16[1,1024,256]{2,1,0:T(8,128)(2,1)S(1)} %get-tuple-element.8.done, f32[1024,256]{1,0:T(8,128)S(1)} %get-tuple-element.9.last, f32[8,128]{1,0:T(8,128)S(1)} %get-tuple-element.10.scale), custom_call_target="tpu_custom_call" | custom-call | tf_op jit(solution)/shard_map/finish/pallas_call | solution.py:309
